TPU v7x, 512 devices: a 8x2x16 block of a 8x16x16 slice. The times are simulated.
512 devices in a mesh: groups: 2 (over y), tok: 16 (over z), head: 8 (over x), row: 2 (over core).
Axes of the slice: x: 8, y: 2, z: 16, core: 2. Of those that a mesh axis runs over, the one named last changes fastest.
The devices are a block of a 8x16x16 slice.
Arguments:
- text: bfloat16 [1024, 8192], P(('groups', 'row'), 'tok'), parts along dimension 0, may hold values from -12 to 12
- q_weight: bfloat16 [8192, 8192], P('tok', 'head'), may hold values from -0.0625 to 0.0625
- out_weight: bfloat16 [8192, 8192], P('head', 'tok'), may hold values from -0.0625 to 0.0625
- keys: bfloat16 [131072, 1024], P(('groups', 'tok'), 'head'), parts along dimension 0, may hold values from -60 to 60
- values: bfloat16 [131072, 1024], P(('groups', 'tok'), 'head'), parts along dimension 0, may hold values from -6 to 6
- gate: float32 [1], replicated, may hold values from 0.3 to 1.5
Outputs:
- result: bfloat16 [1024, 8192], P(('groups', 'row'), 'tok'), parts along dimension 0
There are 2 independent parts, one for each index of `groups`. A program takes and returns all parts, laid end to end along the dimension named above; an argument that names none is the same for every part. Nothing has to cross between parts.
All inputs are finite; a program needn't handle non-finite values.
Results may differ from a plain program's by a relative error of at most 0.015.
Values may be sent and summed in bfloat16 or wider, within the bound.
A program may use at most 64 MiB of HBM per device.

v0:
```python
import jax
import jax.numpy as jnp
from jax import lax
from jax.sharding import PartitionSpec as P

HD = 128
GROUP = 8


def copy_for_each(array, axis):
    devices = lax.axis_size(axis)
    return lax.all_to_all(
        jnp.broadcast_to(array[None], (devices, *array.shape)), axis, 0, 0, tiled=True
    )


def taken_together(array, axis):
    return copy_for_each(array, axis).sum(axis=0)


def cut_along(array, dim, devices):
    lengths = array.shape
    parts = array.reshape(*lengths[:dim], devices, lengths[dim] // devices, *lengths[dim + 1 :])
    return jnp.moveaxis(parts, dim, 0)


def sum_at_owner(array, axis, dim):
    parts = cut_along(array, dim, lax.axis_size(axis))
    arrived = lax.all_to_all(parts, axis, split_axis=0, concat_axis=0, tiled=True)
    return arrived.astype(jnp.float32).sum(axis=0)


def side_by_side(arrays, axis, split_dim, concat_dim, along):
    columns = [a.reshape(*a.shape[:along], -1) for a in arrays]
    both = jnp.concatenate(columns, axis=along)
    out, at, outs = (
        lax.all_to_all(both, axis, split_axis=split_dim, concat_axis=concat_dim, tiled=True),
        0,
        [],
    )
    for a, column in zip(arrays, columns):
        piece = out[..., at : at + column.shape[along]]
        outs.append(piece.reshape(*piece.shape[:along], *a.shape[along:]))
        at += column.shape[along]
    return tuple(outs)


def joined_along(parts, dim):
    parts = jnp.moveaxis(parts, 0, dim)
    lengths = parts.shape
    return parts.reshape(*lengths[:dim], lengths[dim] * lengths[dim + 1], *lengths[dim + 2 :])


def gathered_copies(array, axis, dim):
    return joined_along(copy_for_each(array, axis), dim)


def attend(queries, keys, values, carry):
    tokens = keys.shape[0]
    local_kv = keys.shape[1] // HD
    size = min(512, tokens)
    key_blocks = keys.reshape(tokens // size, size, local_kv, HD)
    value_blocks = values.reshape(tokens // size, size, local_kv, HD)

    def step(state, pair):
        running, total, accum = state
        key_block, value_block = pair
        scores = jnp.einsum(
            "rkgd,skd->krgs", queries, key_block, preferred_element_type=jnp.float32
        )
        newmax = jnp.maximum(running, jnp.max(scores, axis=3))
        weights = jnp.exp(scores - newmax[..., None])
        factor = jnp.exp(running - newmax)
        total = total * factor + jnp.sum(weights, axis=3)
        rounded = weights.astype(jnp.bfloat16)
        accum = accum * factor[..., None] + jnp.einsum(
            "krgs,skd->krgd", rounded, value_block, preferred_element_type=jnp.float32
        )
        return ((newmax, total, accum), None)

    carry, _ = lax.scan(step, carry, (key_blocks, value_blocks))
    return carry


def empty_state(rows, local_kv):
    return (
        jnp.full((local_kv, rows, GROUP), -1e30, jnp.float32),
        jnp.zeros((local_kv, rows, GROUP), jnp.float32),
        jnp.zeros((local_kv, rows, GROUP, HD), jnp.float32),
    )


def finalize(state):
    running, total, accum = state
    outputs = accum / total[..., None]
    local_kv, rows = (outputs.shape[0], outputs.shape[1])
    return (
        jnp.transpose(outputs, (1, 0, 2, 3))
        .reshape(rows, local_kv * GROUP * HD)
        .astype(jnp.bfloat16)
    )


def body(text, q_weight, out_weight, keys, values, gate):
    hidden = text.astype(jnp.float32)
    squares = taken_together(jnp.sum(hidden * hidden, axis=1), "tok")
    features = hidden.shape[1] * lax.axis_size("tok")
    normed = (hidden * lax.rsqrt(squares / features + 1e-05)[:, None]).astype(jnp.bfloat16)
    local_kv = keys.shape[1] // HD
    share_rows = normed.shape[0] // lax.axis_size("tok")
    picked = normed
    projected = sum_at_owner(
        jnp.dot(picked, q_weight, preferred_element_type=jnp.float32).astype(jnp.bfloat16), "tok", 0
    )
    rows = projected.shape[0]
    view = projected.reshape(rows, local_kv, GROUP, HD)
    share_queries = (view / jnp.sqrt(jnp.float32(HD))).astype(jnp.bfloat16)
    queries = lax.all_gather(share_queries, "tok", axis=0, tiled=True)
    running, total, accum = attend(queries, keys, values, empty_state(normed.shape[0], local_kv))
    pieces = tuple(
        (
            part.astype(jnp.float32)
            for part in side_by_side(
                (
                    running[None].astype(jnp.bfloat16),
                    total[None].astype(jnp.bfloat16),
                    accum[None].astype(jnp.bfloat16),
                ),
                "tok",
                2,
                0,
                4,
            )
        )
    )
    piece_max, piece_total, piece_accum = pieces
    newmax = jnp.max(piece_max, axis=0)
    factor = jnp.exp(piece_max - newmax[None])
    merged_total = jnp.sum(piece_total * factor, axis=0)
    merged_accum = jnp.sum(piece_accum * factor[..., None], axis=0)
    share_attended = finalize((newmax, merged_total, merged_accum))
    attended = gathered_copies(share_attended, "tok", 0)
    strength = jnp.tanh(gate[0])
    share_rows = attended.shape[0] // lax.axis_size("head")
    picked = attended
    branch = sum_at_owner(
        jnp.dot(picked, out_weight, preferred_element_type=jnp.float32).astype(jnp.bfloat16),
        "head",
        0,
    )
    offset = lax.axis_index("head") * share_rows
    mine = lax.dynamic_slice_in_dim(hidden, offset, share_rows, 0)
    finished = (mine + strength * branch).astype(jnp.bfloat16)
    return gathered_copies(finished, "head", 0)


def solution(mesh):
    in_specs = (
        P(("groups", "row"), "tok"),
        P("tok", "head"),
        P("head", "tok"),
        P(("groups", "tok"), "head"),
        P(("groups", "tok"), "head"),
        P(),
    )
    out_specs = P(("groups", "row"), "tok")
    return jax.shard_map(body, mesh=mesh, in_specs=in_specs, out_specs=out_specs, check_vma=False)
```

profile of v0, /device:TPU:80, one launch (start us, length us, event | category | flops | bytes accessed | tf_op | source)
XLA Modules:
  0.0 306.5 jit_solution(6369199125377583567)
XLA Ops:
  0.0 1.2 multiply_reduce_fusion.1
  1.2 55.8 %all_to_all.38 = f32[16,1,256]{2,1,0:T(1,128)S(1)} all-to-all(f32[16,1,256]{2,1,0:T(1,128)S(1)} %broadcast_in_dim.17), channel_id=1, replica_groups=mesh['groups'=2,'tok'=16,'head'=8,'row'=2] {'tok'}, dimensions={0} | all-to-all | bytes 32768 | tf_op jit(solution)/shard_map/all_to_all | solution.py:12
  57.0 2.2 convolution_convert_fusion
  59.3 4.0 %all-to-all-start.1 = ((bf16[16,16,1024]{2,1,0:T(8,128)(2,1)}), bf16[16,16,1024]{2,1,0:T(8,128)(2,1)S(1)}, u32[]{:S(2)}, u32[]{:S(2)}) async-start(bf16[16,16,1024]{2,1,0:T(8,128)(2,1)} %bitcast.2), calls=%async_computation.1 | async-start | bytes 1048576 | tf_op jit(solution)/shard_map/all_to_all | solution.py:29
  63.3 26.8 %all-to-all-done.1 = bf16[16,16,1024]{2,1,0:T(8,128)(2,1)S(1)} async-done(((bf16[16,16,1024]{2,1,0:T(8,128)(2,1)}), bf16[16,16,1024]{2,1,0:T(8,128)(2,1)S(1)}, u32[]{:S(2)}, u32[]{:S(2)}) %all-to-all-start.1) | async-done | bytes 524320 | tf_op jit(solution)/shard_map/all_to_all | solution.py:29
  90.2 34.1 %all_gather.3 = bf16[256,1,8,128]{3,2,1,0:T(8,128)(2,1)S(1)} all-gather(bf16[16,1,8,128]{3,2,1,0:T(8,128)(2,1)S(1)} %bitcast.116), channel_id=1, replica_groups=mesh['groups'=2,'tok'=16,'head'=8,'row'=2] {'tok'}, dimensions={0}, use_global_device_ids=true | all-gather | bytes 557056 | tf_op jit(solution)/shard_map/all_gather | solution.py:118
  124.4 64.2 %while.15 = (s32[]{:T(128)}, f32[1,256,8]{1,2,0:T(8,128)S(1)}, f32[1,256,8]{1,2,0:T(8,128)S(1)}, f32[1,256,8,128]{3,1,2,0:T(8,128)S(1)}, bf16[8,512,1,128]{3,1,2...) while((s32[]{:T(128)}, f32[1,256,8]{1,2,0:T(8,128)S(1)}, ...), condition=%wide.region_6.7_spmd.clone, body=%wide.region_3.6_spmd.clone.sunk | while | flops 542912512 | bytes 32375940 | solution.py:81
  124.4 3.5 %bitcast_reduce_fusion.2 = (f32[256,8]{0,1:T(8,128)S(1)}, f32[512,256,8]{1,0,2:T(8,128)}) fusion(bf16[256,1,8,128]{3,0,2,1:T(8,128)(2,1)S(1)} %get-tuple-element.217, bf16[8,512,1,128]{3,1,2,0:T(8,128)(2,1)} %get-tuple-element.216, s32[]{:T(128)} %get-tuple-element.203), kind=kOutput, calls=%fused_computation.1.clone.1 | convolution fusion | flops 269481984 | bytes 4858368 | tf_op jit(solution)/shard_map/while/body/eval_jaxpr/rkgd,skd->krgs/dot_general | solution.py:68
  128.0 3.8 %fusion.44 = f32[1,256,8,128]{3,1,2,0:T(8,128)S(1)} fusion(f32[512,256,8]{1,0,2:T(8,128)} %get-tuple-element.192, f32[256,8]{0,1:T(8,128)S(1)} %bitcast.109, f32[1,256,8,128]{3,1,2,0:T(8,128)S(1)} %get-tuple-element.206, f32[256,8]{0,1:T(8,128)S(1)} %get-tuple-element.193, pred[]{:T(512)S(6)} %compare.3, ...), kind=kOutput, calls=%fused_computation.8.clone.1 | convolution fusion | flops 271319040 | bytes 6439425 | tf_op jit(solution)/shard_map/while/body/eval_jaxpr/krgs,skd->krgd/dot_general | solution.py:76
  131.8 0.6 fusion.43
  132.4 3.5 %bitcast_reduce_fusion.2 = (f32[256,8]{0,1:T(8,128)S(1)}, f32[512,256,8]{1,0,2:T(8,128)}) fusion(bf16[256,1,8,128]{3,0,2,1:T(8,128)(2,1)S(1)} %get-tuple-element.217, bf16[8,512,1,128]{3,1,2,0:T(8,128)(2,1)} %get-tuple-element.216, s32[]{:T(128)} %get-tuple-element.203), kind=kOutput, calls=%fused_computation.1.clone.1 | convolution fusion | flops 269481984 | bytes 4858368 | tf_op jit(solution)/shard_map/while/body/eval_jaxpr/rkgd,skd->krgs/dot_general | solution.py:68
  136.0 3.8 %fusion.44 = f32[1,256,8,128]{3,1,2,0:T(8,128)S(1)} fusion(f32[512,256,8]{1,0,2:T(8,128)} %get-tuple-element.192, f32[256,8]{0,1:T(8,128)S(1)} %bitcast.109, f32[1,256,8,128]{3,1,2,0:T(8,128)S(1)} %get-tuple-element.206, f32[256,8]{0,1:T(8,128)S(1)} %get-tuple-element.193, pred[]{:T(512)S(6)} %compare.3, ...), kind=kOutput, calls=%fused_computation.8.clone.1 | convolution fusion | flops 271319040 | bytes 6439425 | tf_op jit(solution)/shard_map/while/body/eval_jaxpr/krgs,skd->krgd/dot_general | solution.py:76
  139.8 0.6 fusion.43
  140.4 3.5 %bitcast_reduce_fusion.2 = (f32[256,8]{0,1:T(8,128)S(1)}, f32[512,256,8]{1,0,2:T(8,128)}) fusion(bf16[256,1,8,128]{3,0,2,1:T(8,128)(2,1)S(1)} %get-tuple-element.217, bf16[8,512,1,128]{3,1,2,0:T(8,128)(2,1)} %get-tuple-element.216, s32[]{:T(128)} %get-tuple-element.203), kind=kOutput, calls=%fused_computation.1.clone.1 | convolution fusion | flops 269481984 | bytes 4858368 | tf_op jit(solution)/shard_map/while/body/eval_jaxpr/rkgd,skd->krgs/dot_general | solution.py:68
  144.0 3.8 %fusion.44 = f32[1,256,8,128]{3,1,2,0:T(8,128)S(1)} fusion(f32[512,256,8]{1,0,2:T(8,128)} %get-tuple-element.192, f32[256,8]{0,1:T(8,128)S(1)} %bitcast.109, f32[1,256,8,128]{3,1,2,0:T(8,128)S(1)} %get-tuple-element.206, f32[256,8]{0,1:T(8,128)S(1)} %get-tuple-element.193, pred[]{:T(512)S(6)} %compare.3, ...), kind=kOutput, calls=%fused_computation.8.clone.1 | convolution fusion | flops 271319040 | bytes 6439425 | tf_op jit(solution)/shard_map/while/body/eval_jaxpr/krgs,skd->krgd/dot_general | solution.py:76
  147.8 0.6 fusion.43
  148.5 3.5 %bitcast_reduce_fusion.2 = (f32[256,8]{0,1:T(8,128)S(1)}, f32[512,256,8]{1,0,2:T(8,128)}) fusion(bf16[256,1,8,128]{3,0,2,1:T(8,128)(2,1)S(1)} %get-tuple-element.217, bf16[8,512,1,128]{3,1,2,0:T(8,128)(2,1)} %get-tuple-element.216, s32[]{:T(128)} %get-tuple-element.203), kind=kOutput, calls=%fused_computation.1.clone.1 | convolution fusion | flops 269481984 | bytes 4858368 | tf_op jit(solution)/shard_map/while/body/eval_jaxpr/rkgd,skd->krgs/dot_general | solution.py:68
  152.0 3.8 %fusion.44 = f32[1,256,8,128]{3,1,2,0:T(8,128)S(1)} fusion(f32[512,256,8]{1,0,2:T(8,128)} %get-tuple-element.192, f32[256,8]{0,1:T(8,128)S(1)} %bitcast.109, f32[1,256,8,128]{3,1,2,0:T(8,128)S(1)} %get-tuple-element.206, f32[256,8]{0,1:T(8,128)S(1)} %get-tuple-element.193, pred[]{:T(512)S(6)} %compare.3, ...), kind=kOutput, calls=%fused_computation.8.clone.1 | convolution fusion | flops 271319040 | bytes 6439425 | tf_op jit(solution)/shard_map/while/body/eval_jaxpr/krgs,skd->krgd/dot_general | solution.py:76
  155.9 0.6 fusion.43
  156.5 3.5 %bitcast_reduce_fusion.2 = (f32[256,8]{0,1:T(8,128)S(1)}, f32[512,256,8]{1,0,2:T(8,128)}) fusion(bf16[256,1,8,128]{3,0,2,1:T(8,128)(2,1)S(1)} %get-tuple-element.217, bf16[8,512,1,128]{3,1,2,0:T(8,128)(2,1)} %get-tuple-element.216, s32[]{:T(128)} %get-tuple-element.203), kind=kOutput, calls=%fused_computation.1.clone.1 | convolution fusion | flops 269481984 | bytes 4858368 | tf_op jit(solution)/shard_map/while/body/eval_jaxpr/rkgd,skd->krgs/dot_general | solution.py:68
  160.0 3.8 %fusion.44 = f32[1,256,8,128]{3,1,2,0:T(8,128)S(1)} fusion(f32[512,256,8]{1,0,2:T(8,128)} %get-tuple-element.192, f32[256,8]{0,1:T(8,128)S(1)} %bitcast.109, f32[1,256,8,128]{3,1,2,0:T(8,128)S(1)} %get-tuple-element.206, f32[256,8]{0,1:T(8,128)S(1)} %get-tuple-element.193, pred[]{:T(512)S(6)} %compare.3, ...), kind=kOutput, calls=%fused_computation.8.clone.1 | convolution fusion | flops 271319040 | bytes 6439425 | tf_op jit(solution)/shard_map/while/body/eval_jaxpr/krgs,skd->krgd/dot_general | solution.py:76
  163.9 0.6 fusion.43
  164.5 3.5 %bitcast_reduce_fusion.2 = (f32[256,8]{0,1:T(8,128)S(1)}, f32[512,256,8]{1,0,2:T(8,128)}) fusion(bf16[256,1,8,128]{3,0,2,1:T(8,128)(2,1)S(1)} %get-tuple-element.217, bf16[8,512,1,128]{3,1,2,0:T(8,128)(2,1)} %get-tuple-element.216, s32[]{:T(128)} %get-tuple-element.203), kind=kOutput, calls=%fused_computation.1.clone.1 | convolution fusion | flops 269481984 | bytes 4858368 | tf_op jit(solution)/shard_map/while/body/eval_jaxpr/rkgd,skd->krgs/dot_general | solution.py:68
  168.1 3.8 %fusion.44 = f32[1,256,8,128]{3,1,2,0:T(8,128)S(1)} fusion(f32[512,256,8]{1,0,2:T(8,128)} %get-tuple-element.192, f32[256,8]{0,1:T(8,128)S(1)} %bitcast.109, f32[1,256,8,128]{3,1,2,0:T(8,128)S(1)} %get-tuple-element.206, f32[256,8]{0,1:T(8,128)S(1)} %get-tuple-element.193, pred[]{:T(512)S(6)} %compare.3, ...), kind=kOutput, calls=%fused_computation.8.clone.1 | convolution fusion | flops 271319040 | bytes 6439425 | tf_op jit(solution)/shard_map/while/body/eval_jaxpr/krgs,skd->krgd/dot_general | solution.py:76
  171.9 0.6 fusion.43
  172.5 3.5 %bitcast_reduce_fusion.2 = (f32[256,8]{0,1:T(8,128)S(1)}, f32[512,256,8]{1,0,2:T(8,128)}) fusion(bf16[256,1,8,128]{3,0,2,1:T(8,128)(2,1)S(1)} %get-tuple-element.217, bf16[8,512,1,128]{3,1,2,0:T(8,128)(2,1)} %get-tuple-element.216, s32[]{:T(128)} %get-tuple-element.203), kind=kOutput, calls=%fused_computation.1.clone.1 | convolution fusion | flops 269481984 | bytes 4858368 | tf_op jit(solution)/shard_map/while/body/eval_jaxpr/rkgd,skd->krgs/dot_general | solution.py:68
  176.1 3.8 %fusion.44 = f32[1,256,8,128]{3,1,2,0:T(8,128)S(1)} fusion(f32[512,256,8]{1,0,2:T(8,128)} %get-tuple-element.192, f32[256,8]{0,1:T(8,128)S(1)} %bitcast.109, f32[1,256,8,128]{3,1,2,0:T(8,128)S(1)} %get-tuple-element.206, f32[256,8]{0,1:T(8,128)S(1)} %get-tuple-element.193, pred[]{:T(512)S(6)} %compare.3, ...), kind=kOutput, calls=%fused_computation.8.clone.1 | convolution fusion | flops 271319040 | bytes 6439425 | tf_op jit(solution)/shard_map/while/body/eval_jaxpr/krgs,skd->krgd/dot_general | solution.py:76
  179.9 0.6 fusion.43
  180.5 3.5 %bitcast_reduce_fusion.2 = (f32[256,8]{0,1:T(8,128)S(1)}, f32[512,256,8]{1,0,2:T(8,128)}) fusion(bf16[256,1,8,128]{3,0,2,1:T(8,128)(2,1)S(1)} %get-tuple-element.217, bf16[8,512,1,128]{3,1,2,0:T(8,128)(2,1)} %get-tuple-element.216, s32[]{:T(128)} %get-tuple-element.203), kind=kOutput, calls=%fused_computation.1.clone.1 | convolution fusion | flops 269481984 | bytes 4858368 | tf_op jit(solution)/shard_map/while/body/eval_jaxpr/rkgd,skd->krgs/dot_general | solution.py:68
  184.1 3.8 %fusion.44 = f32[1,256,8,128]{3,1,2,0:T(8,128)S(1)} fusion(f32[512,256,8]{1,0,2:T(8,128)} %get-tuple-element.192, f32[256,8]{0,1:T(8,128)S(1)} %bitcast.109, f32[1,256,8,128]{3,1,2,0:T(8,128)S(1)} %get-tuple-element.206, f32[256,8]{0,1:T(8,128)S(1)} %get-tuple-element.193, pred[]{:T(512)S(6)} %compare.3, ...), kind=kOutput, calls=%fused_computation.8.clone.1 | convolution fusion | flops 271319040 | bytes 6439425 | tf_op jit(solution)/shard_map/while/body/eval_jaxpr/krgs,skd->krgd/dot_general | solution.py:76
  187.9 0.6 fusion.43
  188.6 0.4 copy.72
  188.9 0.4 copy.73
  189.3 0.6 copy.89
  189.9 0.9 pad_maximum_fusion
  190.9 47.4 %all_to_all.39 = bf16[1,1,256,8,130]{4,3,1,0,2:T(8,128)(2,1)S(1)} all-to-all(bf16[1,1,256,8,130]{4,3,1,0,2:T(8,128)(2,1)S(1)} %pad_maximum_fusion), channel_id=1, replica_groups=mesh['groups'=2,'tok'=16,'head'=8,'row'=2] {'tok'}, dimensions={2} | all-to-all | bytes 1064960 | tf_op jit(solution)/shard_map/all_to_all | solution.py:37
  238.2 0.4 fusion.31
  238.7 0.8 copy.80
  239.6 0.8 copy.81
  240.6 0.1 copy.75
  240.7 0.5 multiply_reduce_fusion
  241.2 0.1 divide_convert_fusion
  241.4 29.5 %all_to_all.40 = bf16[16,16,1024]{2,1,0:T(8,128)(2,1)S(1)} all-to-all(bf16[16,16,1024]{2,1,0:T(8,128)(2,1)S(1)} %broadcast_in_dim.18), channel_id=1, replica_groups=mesh['groups'=2,'tok'=16,'head'=8,'row'=2] {'tok'}, dimensions={0} | all-to-all | bytes 1048576 | tf_op jit(solution)/shard_map/all_to_all | solution.py:12
  270.9 2.4 convolution_convert_fusion.1
  273.2 7.6 %all-to-all-start.4 = ((bf16[8,32,512]{2,1,0:T(8,128)(2,1)}), bf16[8,32,512]{2,1,0:T(8,128)(2,1)S(1)}, u32[]{:S(2)}, u32[]{:S(2)}) async-start(bf16[8,32,512]{2,1,0:T(8,128)(2,1)} %bitcast.13), calls=%async_computation.4 | async-start | bytes 524288 | tf_op jit(solution)/shard_map/all_to_all | solution.py:29
  281.6 10.8 %all-to-all-done.4 = bf16[8,32,512]{2,1,0:T(8,128)(2,1)S(1)} async-done(((bf16[8,32,512]{2,1,0:T(8,128)(2,1)}), bf16[8,32,512]{2,1,0:T(8,128)(2,1)S(1)}, u32[]{:S(2)}, u32[]{:S(2)}) %all-to-all-start.4) | async-done | bytes 262176 | tf_op jit(solution)/shard_map/all_to_all | solution.py:29
  292.5 13.3 %all_to_all.41 = bf16[8,32,512]{2,1,0:T(8,128)(2,1)S(1)} all-to-all(bf16[8,32,512]{2,1,0:T(8,128)(2,1)S(1)} %broadcast_in_dim.19), channel_id=1, replica_groups=mesh['groups'=2,'tok'=16,'head'=8,'row'=2] {'head'}, dimensions={0} | all-to-all | bytes 524288 | tf_op jit(solution)/shard_map/all_to_all | solution.py:12
  305.8 0.7 copy.105
  (66 shorter events, 0.9 us)
Async XLA Ops:
  0.0 57.0 %copy-start = (bf16[512,1024]{1,0:T(8,128)(2,1)S(1)}, bf16[512,1024]{1,0:T(8,128)(2,1)}, u32[]{:S(2)}) copy-start(bf16[512,1024]{1,0:T(8,128)(2,1)} %param.9) | copy-start | bytes 3145732
  59.3 30.8 %all-to-all-start.1 = ((bf16[16,16,1024]{2,1,0:T(8,128)(2,1)}), bf16[16,16,1024]{2,1,0:T(8,128)(2,1)S(1)}, u32[]{:S(2)}, u32[]{:S(2)}) async-start(bf16[16,16,1024]{2,1,0:T(8,128)(2,1)} %bitcast.2), calls=%async_computation.1 | async-start | bytes 1048576 | tf_op jit(solution)/shard_map/all_to_all | solution.py:29
  127.9 3.8 %copy-start.1 = (f32[512,256,8]{1,0,2:T(8,128)S(1)}, f32[512,256,8]{1,0,2:T(8,128)}, u32[]{:S(2)}) copy-start(f32[512,256,8]{1,0,2:T(8,128)} %get-tuple-element.192) | copy-start | bytes 12582916 | tf_op jit(solution)/shard_map/while
  136.0 3.8 %copy-start.1 = (f32[512,256,8]{1,0,2:T(8,128)S(1)}, f32[512,256,8]{1,0,2:T(8,128)}, u32[]{:S(2)}) copy-start(f32[512,256,8]{1,0,2:T(8,128)} %get-tuple-element.192) | copy-start | bytes 12582916 | tf_op jit(solution)/shard_map/while
  144.0 3.8 %copy-start.1 = (f32[512,256,8]{1,0,2:T(8,128)S(1)}, f32[512,256,8]{1,0,2:T(8,128)}, u32[]{:S(2)}) copy-start(f32[512,256,8]{1,0,2:T(8,128)} %get-tuple-element.192) | copy-start | bytes 12582916 | tf_op jit(solution)/shard_map/while
  152.0 3.8 %copy-start.1 = (f32[512,256,8]{1,0,2:T(8,128)S(1)}, f32[512,256,8]{1,0,2:T(8,128)}, u32[]{:S(2)}) copy-start(f32[512,256,8]{1,0,2:T(8,128)} %get-tuple-element.192) | copy-start | bytes 12582916 | tf_op jit(solution)/shard_map/while
  160.0 3.8 %copy-start.1 = (f32[512,256,8]{1,0,2:T(8,128)S(1)}, f32[512,256,8]{1,0,2:T(8,128)}, u32[]{:S(2)}) copy-start(f32[512,256,8]{1,0,2:T(8,128)} %get-tuple-element.192) | copy-start | bytes 12582916 | tf_op jit(solution)/shard_map/while
  168.0 3.8 %copy-start.1 = (f32[512,256,8]{1,0,2:T(8,128)S(1)}, f32[512,256,8]{1,0,2:T(8,128)}, u32[]{:S(2)}) copy-start(f32[512,256,8]{1,0,2:T(8,128)} %get-tuple-element.192) | copy-start | bytes 12582916 | tf_op jit(solution)/shard_map/while
  176.1 3.8 %copy-start.1 = (f32[512,256,8]{1,0,2:T(8,128)S(1)}, f32[512,256,8]{1,0,2:T(8,128)}, u32[]{:S(2)}) copy-start(f32[512,256,8]{1,0,2:T(8,128)} %get-tuple-element.192) | copy-start | bytes 12582916 | tf_op jit(solution)/shard_map/while
  184.1 3.8 %copy-start.1 = (f32[512,256,8]{1,0,2:T(8,128)S(1)}, f32[512,256,8]{1,0,2:T(8,128)}, u32[]{:S(2)}) copy-start(f32[512,256,8]{1,0,2:T(8,128)} %get-tuple-element.192) | copy-start | bytes 12582916 | tf_op jit(solution)/shard_map/while
  238.2 42.6 %copy-start.2 = (bf16[256,512]{1,0:T(8,128)(2,1)S(1)}, bf16[256,512]{1,0:T(8,128)(2,1)}, u32[]{:S(2)}) copy-start(bf16[256,512]{1,0:T(8,128)(2,1)} %param.8) | copy-start | bytes 786436
  273.2 19.2 %all-to-all-start.4 = ((bf16[8,32,512]{2,1,0:T(8,128)(2,1)}), bf16[8,32,512]{2,1,0:T(8,128)(2,1)S(1)}, u32[]{:S(2)}, u32[]{:S(2)}) async-start(bf16[8,32,512]{2,1,0:T(8,128)(2,1)} %bitcast.13), calls=%async_computation.4 | async-start | bytes 524288 | tf_op jit(solution)/shard_map/all_to_all | solution.py:29
where the time goes:
time: 307 us
  blocking collectives  180 us (59%)
  matrix products  63.6 us (21%)
  waiting for transfers between devices  37.6 us (12%)
  starting transfers between devices  11.7 us (4%)
  other arithmetic  8.17 us (3%)
  local copies, waits for them, and re-layouts  4.22 us (1%)
    all_to_all x3, blocking collectives, copy_for_each(): lax.all_to_all(jnp.broadcast_to(array[None], (devices, *array.shape)), ax...  98.6 us
    all_to_all x1, blocking collectives, side_by_side(): lax.all_to_all(both, axis, split_axis=split_dim, concat_axis=concat_dim,...  47.4 us
    all_to_all x2, waiting for transfers between devices, sum_at_owner(): lax.all_to_all(parts, axis, split_axis=0, concat_axis=0, tiled=True)  37.6 us
    all_gather x1, blocking collectives, body(): queries = lax.all_gather(share_queries, 'tok', axis=0, tiled=True)  34.1 us
    dot_general x8, matrix products, step(): jnp.einsum('krgs,skd->krgd', rounded, value_block, preferred_element_type...  30.6 us
    dot_general x8, matrix products, step(): jnp.einsum('rkgd,skd->krgs', queries, key_block, preferred_element_type=j...  28.4 us
    all_to_all x2, starting transfers between devices, sum_at_owner(): lax.all_to_all(parts, axis, split_axis=0, concat_axis=0, tiled=True)  11.7 us
  transfers between devices with their start and end apart: 2, of which 2 were waited for; matrix products, arithmetic and copies ran while one was open for 0% of the time, Pallas kernels for 0%

commit v1 on v0

v1 whole, which is shorter than its diff:
```python
import functools
import math

import jax
import jax.numpy as jnp
from jax import lax
from jax.experimental import pallas as pl
from jax.experimental.pallas import tpu as pltpu
from jax.sharding import PartitionSpec as P

HD = 128
MESH = pl.DeviceIdType.MESH
F32 = jnp.float32
BF16 = jnp.bfloat16
NT = (((1,), (1,)), ((), ()))
DIRS = (1, -1)


class Tree:
    def __init__(self, half, step):
        self.half = half
        self.relays = tuple(range(0, half, step))

    def up(self, d):
        return max(r for r in self.relays if r < d)

    def below(self, r, sign):
        if r not in self.relays:
            return []
        return [d for d in range(self.far(sign), 0, -1) if self.up(d) == r]

    def far(self, sign):
        return self.half if sign == 1 else self.half - 1

    def hops(self):
        return {d - self.up(d) for d in range(1, self.half + 1)}


def split(x):
    high = x.astype(BF16).astype(F32)
    rest = x - high
    middle = rest.astype(BF16).astype(F32)
    return high, middle, rest - middle


def kernel(
    cfg,
    text_hbm, q_hbm, o_hbm, k_hbm, v_hbm, gate_ref,
    out_ref,
    text_v, q_v, o_v, k_v, v_v, vt_v, load_sem,
    part, ps_out, ps_in, ps_send, ps_recv,
    q_own, q_in, q_send, q_recv,
    acc_loc, stat_loc, st_out, st_in, st_send, st_recv,
    at_own, at_in, at_send, at_recv,
    own_x, x_out, x_in, x_send, x_recv,
    fin, f_send, f_recv,
):
    n, m, half, trees, block, unroll = cfg
    tree_p, tree_q, tree_s, tree_a = trees
    z = lax.axis_index("tok")
    x = lax.axis_index("head")
    rows = text_hbm.shape[0]
    depth = text_hbm.shape[1]
    piece = rows // n
    wide = q_hbm.shape[1]
    heads = wide // HD
    nq = heads * piece
    tokens = k_hbm.shape[0]
    scale_in = 1.0 / (depth * n)

    loads = [
        pltpu.make_async_copy(src, dst, load_sem.at[i])
        for i, (src, dst) in enumerate(
            ((text_hbm, text_v), (q_hbm, q_v), (v_hbm, v_v), (k_hbm, k_v), (o_hbm, o_v))
        )
    ]
    for c in loads:
        c.start()

    reach = sorted({(s * h) % n for t in trees for h in t.hops() for s in DIRS} - {0})
    barrier = pltpu.get_barrier_semaphore()
    for h in reach:
        pl.semaphore_signal(
            barrier, inc=1, device_id={"tok": lax.rem(z + h, n)}, device_id_type=MESH
        )
    for j in range(1, m):
        pl.semaphore_signal(
            barrier, inc=1, device_id={"head": lax.rem(x + j, m)}, device_id_type=MESH
        )

    def at(sign, d):
        return lax.rem(z + sign * d + 2 * n, n)

    def rows_of(p):
        return pl.ds(pl.multiple_of(p * piece, piece), piece)

    def along_z(src, dst, send, recv, sign, hop):
        return pltpu.make_async_remote_copy(
            src_ref=src, dst_ref=dst, send_sem=send, recv_sem=recv,
            device_id={"tok": at(sign, hop)}, device_id_type=MESH,
        )

    def lane(i):
        return pl.ds(i * nq, nq)

    loads[0].wait()
    loads[1].wait()
    text = text_v[...]
    hidden = text.astype(F32)
    first = lax.broadcasted_iota(jnp.int32, (rows, HD), 1) == 0
    squares = jnp.sum(hidden * hidden, axis=1, keepdims=True)
    part[:, wide:] = jnp.where(first, jnp.broadcast_to(squares, (rows, HD)), 0.0)
    cut = 256 if wide % 256 == 0 else 128
    for c in range(wide // cut):
        part[:, c * cut : (c + 1) * cut] = jnp.dot(
            text, q_v[:, c * cut : (c + 1) * cut], preferred_element_type=F32
        )

    def ps_copy(i, d):
        sign = DIRS[i]
        return along_z(
            ps_out.at[i, d], ps_in.at[i, d], ps_send.at[i, d], ps_recv.at[i, d],
            sign, d - tree_p.up(d),
        )

    lanes = lax.broadcasted_iota(jnp.int32, (piece, HD), 1)

    def gather_part(i_list, r, owner):
        main = part[rows_of(owner), :wide]
        tail = part[rows_of(owner), wide:]
        for i in i_list:
            for d in tree_p.below(r, DIRS[i]):
                ps_copy(i, d).wait_recv()
                main = main + ps_in[i, d, :, :wide].astype(F32)
                tail = tail + ps_in[i, d, :, wide:].astype(F32)
        return main, jnp.sum(tail, axis=1, keepdims=True)

    def send_part(i, d):
        main, sums = gather_part([i], d, at(DIRS[i], d))
        high = sums.astype(BF16).astype(F32)
        low = sums - high
        ps_out[i, d, :, :wide] = main.astype(BF16)
        ps_out[i, d, :, wide:] = jnp.where(
            lanes == 0, high, jnp.where(lanes == 1, low, 0.0)
        ).astype(BF16)
        ps_copy(i, d).start()

    pl.semaphore_wait(barrier, len(reach) + m - 1)

    todo = [(d, i) for d in range(half, 0, -1) for i in (0, 1) if d <= tree_p.far(DIRS[i])]
    leaves = [(d, i) for d, i in todo if not tree_p.below(d, DIRS[i])]
    inner = [(d, i) for d, i in todo if tree_p.below(d, DIRS[i])]
    for d, i in leaves:
        send_part(i, d)

    loads[2].wait()
    for c in range(0, tokens, block):
        vt_v[:, c : c + block] = v_v[c : c + block, :].astype(F32).T.astype(BF16)

    for d, i in inner:
        send_part(i, d)

    main, sums = gather_part([0, 1], 0, z)
    norm = lax.rsqrt(sums * scale_in + 1e-05) * (math.log2(math.e) / math.sqrt(HD))
    queries = (main * norm).astype(BF16)
    for g in range(heads):
        q_own[g * piece : (g + 1) * piece, :] = queries[:, g * HD : (g + 1) * HD]

    def q_copy(i, d):
        up = tree_q.up(d)
        src = q_own if up == 0 else q_in.at[up, lane(i)]
        return along_z(
            src, q_in.at[d, lane(i)], q_send.at[i, d], q_recv.at[i, d], DIRS[i], d - up
        )

    def forward_q(r):
        for i in (0, 1):
            if r:
                if r > tree_q.far(DIRS[i]):
                    continue
                q_copy(i, r).wait_recv()
            for d in tree_q.below(r, DIRS[i]):
                q_copy(i, d).start()

    forward_q(0)
    loads[3].wait()

    def attend(q):
        width = q.shape[0]

        def step(b, state):
            running, total, accum = state
            for u in range(unroll):
                start = pl.multiple_of((b * unroll + u) * block, block)
                scores = lax.dot_general(
                    k_v[pl.ds(start, block), :], q, NT, preferred_element_type=F32
                )
                newmax = jnp.maximum(running, jnp.max(scores, axis=0, keepdims=True))
                weights = jnp.exp2(scores - newmax)
                factor = jnp.exp2(running - newmax)
                total = total * factor + jnp.sum(weights, axis=0, keepdims=True)
                accum = accum * factor + jnp.dot(
                    vt_v[:, pl.ds(start, block)], weights.astype(BF16),
                    preferred_element_type=F32,
                )
                running = newmax
            return running, total, accum

        start = (
            jnp.full((1, width), -1e30, F32),
            jnp.zeros((1, width), F32),
            jnp.zeros((HD, width), F32),
        )
        return lax.fori_loop(0, tokens // (block * unroll), step, start)

    def st_copy(i, e):
        return along_z(
            st_out.at[i, e], st_in.at[i, e], st_send.at[i, e], st_recv.at[i, e],
            DIRS[i], e - tree_s.up(e),
        )

    stat_row = lax.broadcasted_iota(jnp.int32, (16, nq), 0)

    def send_state(i, e, running, total, accum):
        st_out[i, e, :HD, :] = accum.astype(BF16)
        stats = jnp.zeros((16, nq), F32)
        for k, term in enumerate(split(running) + split(total)):
            stats = jnp.where(stat_row == k, term, stats)
        st_out[i, e, HD:, :] = stats.astype(BF16)
        st_copy(i, e).start()

    def merged(i_list, e, d, i_own):
        running = stat_loc[i_own, d, 0:1, :]
        total = stat_loc[i_own, d, 1:2, :]
        accum = acc_loc[i_own, d]
        for i in i_list:
            for c in tree_s.below(e, DIRS[i]):
                st_copy(i, c).wait_recv()
                stats = st_in[i, c, HD:, :].astype(F32)
                peer_max = stats[0:1] + stats[1:2] + stats[2:3]
                peer_total = stats[3:4] + stats[4:5] + stats[5:6]
                newmax = jnp.maximum(running, peer_max)
                mine, theirs = jnp.exp2(running - newmax), jnp.exp2(peer_max - newmax)
                total = total * mine + peer_total * theirs
                accum = accum * mine + st_in[i, c, :HD, :].astype(F32) * theirs
                running = newmax
        return running, total, accum

    def finish_state(d):
        e = half - d
        for i in (0, 1):
            if 1 <= e <= tree_s.far(DIRS[i]) and tree_s.below(e, DIRS[i]):
                send_state(i, e, *merged([i], e, d, i))

    def attend_piece(d):
        both = 0 < d < half
        q = q_own[...] if d == 0 else (q_in[d] if both else q_in[d, 0:nq, :])
        running, total, accum = attend(q)
        e = half - d
        for i in (0, 1) if both else (0,):
            cols = slice(i * nq, (i + 1) * nq)
            r, t, a = running[:, cols], total[:, cols], accum[:, cols]
            if e and not tree_s.below(e, DIRS[i]):
                send_state(i, e, r, t, a)
            else:
                stat_loc[i, d, 0:1, :] = r
                stat_loc[i, d, 1:2, :] = t
                acc_loc[i, d] = a

    late = []
    forwarded = {0}
    for d in range(half + 1):
        for r in (d, d + 1):
            if r in tree_q.relays and r not in forwarded:
                forward_q(r)
                forwarded.add(r)
        if d and d not in forwarded:
            for i in (0, 1):
                if d <= tree_q.far(DIRS[i]):
                    q_copy(i, d).wait_recv()
        attend_piece(d)
        while late:
            finish_state(late.pop())
        late.append(d)

    _, total, accum = merged([0, 1], 0, half, 0)
    attended = (accum / total).T
    for g in range(heads):
        at_own[:, g * HD : (g + 1) * HD] = attended[g * piece : (g + 1) * piece, :].astype(BF16)

    def at_copy(i, d):
        up = tree_a.up(d)
        span = pl.ds(i * piece, piece)
        src = at_own if up == 0 else at_in.at[up, span]
        return along_z(
            src, at_in.at[d, span], at_send.at[i, d], at_recv.at[i, d], DIRS[i], d - up
        )

    def forward_a(r):
        for i in (0, 1):
            if r:
                if r > tree_a.far(DIRS[i]):
                    continue
                at_copy(i, r).wait_recv()
            for d in tree_a.below(r, DIRS[i]):
                at_copy(i, d).start()

    def place(i, d):
        p = lax.rem(z - DIRS[i] * d + half + n, n)
        which = lax.div(p, m)
        owner = lax.rem(p, m)
        return which, owner, lax.rem(x - owner + m, m)

    def x_copy(i, d):
        which, owner, j = place(i, d)
        return pltpu.make_async_remote_copy(
            src_ref=x_out.at[i, d], dst_ref=x_in.at[which, j],
            send_sem=x_send.at[i, d], recv_sem=x_recv.at[which, j],
            device_id={"head": owner}, device_id_type=MESH,
        )

    def project(d):
        both = 0 < d < half
        a = at_own[...] if d == 0 else (at_in[d] if both else at_in[d, 0:piece, :])
        branch = jnp.dot(a, o_v[...], preferred_element_type=F32)
        for i in (0, 1) if both else (0,):
            term = branch[i * piece : (i + 1) * piece, :]
            which, owner, j = place(i, d)

            @pl.when(j == 0)
            def _():
                own_x[which] = term

            @pl.when(j != 0)
            def _():
                x_out[i, d] = term.astype(BF16)
                x_copy(i, d).start()

    def f_copy(which, j):
        p = x + which * m
        return pltpu.make_async_remote_copy(
            src_ref=fin.at[which], dst_ref=out_ref.at[rows_of(p)],
            send_sem=f_send.at[which, j], recv_sem=f_recv.at[which, j],
            device_id={"head": lax.rem(x + j, m)}, device_id_type=MESH,
        )

    strength = jnp.tanh(jnp.full((piece, depth), gate_ref[0], F32))

    def finish_rows(which):
        branch = own_x[which]
        for j in range(1, m):
            pltpu.make_async_remote_copy(
                src_ref=fin.at[0], dst_ref=x_in.at[which, j],
                send_sem=f_send.at[0, 0], recv_sem=x_recv.at[which, j],
                device_id={"head": lax.rem(x + j, m)}, device_id_type=MESH,
            ).wait_recv()
            branch = branch + x_in[which, j].astype(F32)
        p = x + which * m
        done = (text_v[rows_of(p), :].astype(F32) + strength * branch).astype(BF16)
        fin[which] = done
        for j in range(1, m):
            f_copy(which, j).start()
        out_ref[rows_of(p), :] = done

    loads[4].wait()
    forward_a(0)
    forwarded = {0}
    early = lax.div(lax.rem(z + half - x + n + half // 2, n), half + 1)
    for d in range(half + 1):
        for r in (d, d + 1):
            if r in tree_a.relays and r not in forwarded:
                forward_a(r)
                forwarded.add(r)
        if d and d not in forwarded:
            for i in (0, 1):
                if d <= tree_a.far(DIRS[i]):
                    at_copy(i, d).wait_recv()
        project(d)
        if d == half - 1:
            finish_rows(early)
    finish_rows(1 - early)

    for j in range(1, m):
        for which in (0, 1):
            p = lax.rem(x - j + m, m) + which * m
            pltpu.make_async_remote_copy(
                src_ref=fin.at[which], dst_ref=out_ref.at[rows_of(p)],
                send_sem=f_send.at[which, j], recv_sem=f_recv.at[which, j],
                device_id={"head": lax.rem(x + j, m)}, device_id_type=MESH,
            ).wait_recv()

    for i in (0, 1):
        for d in range(1, tree_p.far(DIRS[i]) + 1):
            ps_copy(i, d).wait_send()
            q_copy(i, d).wait_send()
            st_copy(i, d).wait_send()
            at_copy(i, d).wait_send()
        for d in range(0, half + 1):
            if i == 1 and d in (0, half):
                continue
            _, _, j = place(i, d)

            @pl.when(j != 0)
            def _():
                x_copy(i, d).wait_send()

    for which in (0, 1):
        for j in range(1, m):
            f_copy(which, j).wait_send()


STEPS = (2, 2, 2, 2)
BLOCK = 512
UNROLL = 4


def body(text, q_weight, out_weight, keys, values, gate):
    n, m = lax.axis_size("tok"), lax.axis_size("head")
    half = n // 2
    assert n == 2 * m and keys.shape[1] == HD
    rows, depth = text.shape
    wide = q_weight.shape[1]
    tokens = keys.shape[0]
    piece = rows // n
    heads = wide // HD
    nq = heads * piece
    block = min(BLOCK, tokens)
    unroll = min(UNROLL, tokens // block)
    trees = tuple(Tree(half, s) for s in STEPS)
    vm, dma = pltpu.VMEM, pltpu.SemaphoreType.DMA
    slots = (2, half + 1)
    scratch = [
        vm((rows, depth), BF16), vm((depth, wide), BF16), vm((wide, depth), BF16),
        vm((tokens, HD), BF16), vm((tokens, HD), BF16), vm((HD, tokens), BF16), dma((5,)),
        vm((rows, wide + HD), F32),
        vm((*slots, piece, wide + HD), BF16), vm((*slots, piece, wide + HD), BF16), dma(slots), dma(slots),
        vm((nq, HD), BF16), vm((half + 1, 2 * nq, HD), BF16), dma(slots), dma(slots),
        vm((*slots, HD, nq), F32), vm((*slots, 8, nq), F32),
        vm((*slots, HD + 16, nq), BF16), vm((*slots, HD + 16, nq), BF16), dma(slots), dma(slots),
        vm((piece, wide), BF16), vm((half + 1, 2 * piece, wide), BF16), dma(slots), dma(slots),
        vm((2, piece, depth), F32), vm((*slots, piece, depth), BF16), vm((2, m, piece, depth), BF16),
        dma(slots), dma((2, m)),
        vm((2, piece, depth), BF16), dma((2, m)), dma((2, m)),
    ]
    hbm = pl.BlockSpec(memory_space=pl.ANY)
    return pl.pallas_call(
        functools.partial(kernel, (n, m, half, trees, block, unroll)),
        out_shape=jax.ShapeDtypeStruct((rows, depth), BF16),
        in_specs=[hbm] * 5 + [pl.BlockSpec(memory_space=pltpu.SMEM)],
        out_specs=pl.BlockSpec(memory_space=pltpu.VMEM),
        scratch_shapes=scratch,
        compiler_params=pltpu.CompilerParams(
            collective_id=0, has_side_effects=True, vmem_limit_bytes=48 * 1024 * 1024
        ),
    )(text, q_weight, out_weight, keys, values, gate)


def solution(mesh):
    in_specs = (
        P(("groups", "row"), "tok"),
        P("tok", "head"),
        P("head", "tok"),
        P(("groups", "tok"), "head"),
        P(("groups", "tok"), "head"),
        P(),
    )
    out_specs = P(("groups", "row"), "tok")
    return jax.shard_map(body, mesh=mesh, in_specs=in_specs, out_specs=out_specs, check_vma=False)
```

time: 307 us -> 133 us (0.43)
  blocking collectives: 180 us -> 0 us
  Pallas kernels: 0 us -> 126 us
  matrix products: 63.6 us -> 0 us
  waiting for transfers between devices: 37.6 us -> 0 us
  starting transfers between devices: 11.7 us -> 0 us
  other arithmetic: 8.17 us -> 0 us
    all_to_all x4 -> x0, blocking collectives: 146 us -> none  [the longest x3 98.6 us: copy_for_each(): lax.all_to_all(jnp.broadcast_to(array[None], (devices, *array.shape)), ax...]
    pallas_call x0 -> x1, Pallas kernels: none -> 126 us  [body(): pl.pallas_call(functools.partial(kernel, (n, m, half, trees, block, unrol...]
    dot_general x18 -> x0, matrix products: 63.6 us -> none  [the longest x8 30.6 us: step(): jnp.einsum('krgs,skd->krgd', rounded, value_block, preferred_element_type...]
    all_to_all x2 -> x0, waiting for transfers between devices: 37.6 us -> none  [sum_at_owner(): lax.all_to_all(parts, axis, split_axis=0, concat_axis=0, tiled=True)]
    all_gather x1 -> x0, blocking collectives: 34.1 us -> none  [body(): queries = lax.all_gather(share_queries, 'tok', axis=0, tiled=True)]
    all_to_all x2 -> x0, starting transfers between devices: 11.7 us -> none  [sum_at_owner(): lax.all_to_all(parts, axis, split_axis=0, concat_axis=0, tiled=True)]
    reduce_sum x14 -> x0, other arithmetic: 6.43 us -> none  [the longest x8 4.61 us: step(): total = total * factor + jnp.sum(weights, axis=3)]
    unnamed x11, local copies, waits for them, and re-layouts: 2.57 us -> 6.55 us
  transfers between devices with their start and end apart: 2 -> 0, of which waited for: 2 -> 0; matrix products, arithmetic and copies ran while one was open for 0% -> 0% of each run, Pallas kernels for 0% -> 0%
where the time goes in v1:
time: 133 us
  Pallas kernels  126 us (95%)
  local copies, waits for them, and re-layouts  6.55 us (5%)
    pallas_call x1, Pallas kernels, body(): pl.pallas_call(functools.partial(kernel, (n, m, half, trees, block, unrol...  126 us
    unnamed x11, local copies, waits for them, and re-layouts  6.55 us

profile of v1, /device:TPU:80, one launch (start us, length us, event | category | flops | bytes accessed | tf_op | source)
XLA Modules:
  0.0 132.9 jit_solution(12817192600355936034)
XLA Ops:
  0.7 0.0 copy-start
  0.7 1.2 copy-done
  1.9 0.0 copy-start.1
  1.9 1.2 copy-done.1
  3.1 0.0 copy-start.2
  3.1 1.2 copy-done.2
  4.3 0.0 copy-start.3
  4.3 1.2 copy-done.3
  5.6 0.0 copy-start.4
  5.6 0.9 copy-done.4
  6.5 125.7 %shard_map.64 = bf16[256,512]{1,0:T(8,128)(2,1)S(1)} custom-call(bf16[256,512]{1,0:T(8,128)(2,1)S(1)} %copy-done.4, bf16[512,1024]{1,0:T(8,128)(2,1)S(1)} %copy-done, bf16[1024,512]{1,0:T(8,128)(2,1)S(1)} %copy-done.1, bf16[4096,128]{1,0:T(8,128)(2,1)S(1)} %copy-done.2, bf16[4096,128]{1,0:T(8,128)(2,1)S(1)} %copy-done.3, f32[1]{0:T(128)S(6)} %copy.8.gate_ref), custom_call_target="tpu_custom_call" | custom-call | tf_op jit(solution)/shard_map/pallas_call | solution.py:446
  132.2 0.7 copy.9
Async XLA Ops:
  0.7 1.2 copy-start
  1.9 1.2 copy-start.1
  3.1 1.2 copy-start.2
  4.3 1.2 copy-start.3
  5.6 0.9 copy-start.4

commit v2 on v1

--- a/solution.py
+++ b/solution.py
@@ -47,7 +47,7 @@
     cfg,
     text_hbm, q_hbm, o_hbm, k_hbm, v_hbm, gate_ref,
     out_ref,
-    text_v, q_v, o_v, k_v, v_v, vt_v, load_sem,
+    text_v, q_v, o_v, k_v, v_v, vt_v, load_sem, scores_v,
     part, ps_out, ps_in, ps_send, ps_recv,
     q_own, q_in, q_send, q_recv,
     acc_loc, stat_loc, st_out, st_in, st_send, st_recv,
@@ -55,7 +55,7 @@
     own_x, x_out, x_in, x_send, x_recv,
     fin, f_send, f_recv,
 ):
-    n, m, half, trees, block, unroll = cfg
+    n, m, half, trees, block = cfg
     tree_p, tree_q, tree_s, tree_a = trees
     z = lax.axis_index("tok")
     x = lax.axis_index("head")
@@ -74,8 +74,8 @@
             ((text_hbm, text_v), (q_hbm, q_v), (v_hbm, v_v), (k_hbm, k_v), (o_hbm, o_v))
         )
     ]
-    for c in loads:
-        c.start()
+    loads[0].start()
+    loads[1].start()
 
     reach = sorted({(s * h) % n for t in trees for h in t.hops() for s in DIRS} - {0})
     barrier = pltpu.get_barrier_semaphore()
@@ -105,6 +105,8 @@
 
     loads[0].wait()
     loads[1].wait()
+    for c in loads[2:]:
+        c.start()
     text = text_v[...]
     hidden = text.astype(F32)
     first = lax.broadcasted_iota(jnp.int32, (rows, HD), 1) == 0
@@ -153,10 +155,6 @@
     for d, i in leaves:
         send_part(i, d)
 
-    loads[2].wait()
-    for c in range(0, tokens, block):
-        vt_v[:, c : c + block] = v_v[c : c + block, :].astype(F32).T.astype(BF16)
-
     for d, i in inner:
         send_part(i, d)
 
@@ -183,35 +181,29 @@
                 q_copy(i, d).start()
 
     forward_q(0)
+    loads[2].wait()
+    for c in range(0, tokens, block):
+        vt_v[:, c : c + block] = v_v[c : c + block, :].astype(F32).T.astype(BF16)
     loads[3].wait()
 
     def attend(q):
         width = q.shape[0]
-
-        def step(b, state):
-            running, total, accum = state
-            for u in range(unroll):
-                start = pl.multiple_of((b * unroll + u) * block, block)
-                scores = lax.dot_general(
-                    k_v[pl.ds(start, block), :], q, NT, preferred_element_type=F32
-                )
-                newmax = jnp.maximum(running, jnp.max(scores, axis=0, keepdims=True))
-                weights = jnp.exp2(scores - newmax)
-                factor = jnp.exp2(running - newmax)
-                total = total * factor + jnp.sum(weights, axis=0, keepdims=True)
-                accum = accum * factor + jnp.dot(
-                    vt_v[:, pl.ds(start, block)], weights.astype(BF16),
-                    preferred_element_type=F32,
-                )
-                running = newmax
-            return running, total, accum
-
-        start = (
-            jnp.full((1, width), -1e30, F32),
-            jnp.zeros((1, width), F32),
-            jnp.zeros((HD, width), F32),
-        )
-        return lax.fori_loop(0, tokens // (block * unroll), step, start)
+        cols = slice(0, width)
+        top = jnp.full((8, width), -1e30, F32)
+        for b in range(0, tokens, block):
+            scores = lax.dot_general(k_v[b : b + block, :], q, NT, preferred_element_type=F32)
+            scores_v[b : b + block, cols] = scores
+            top = jnp.maximum(top, jnp.max(scores.reshape(block // 8, 8, width), axis=0))
+        running = jnp.max(top, axis=0, keepdims=True)
+        sums = jnp.zeros((8, width), F32)
+        accum = jnp.zeros((HD, width), F32)
+        for b in range(0, tokens, block):
+            weights = jnp.exp2(scores_v[b : b + block, cols] - running)
+            sums = sums + jnp.sum(weights.reshape(block // 8, 8, width), axis=0)
+            accum = accum + jnp.dot(
+                vt_v[:, b : b + block], weights.astype(BF16), preferred_element_type=F32
+            )
+        return running, jnp.sum(sums, axis=0, keepdims=True), accum
 
     def st_copy(i, e):
         return along_z(
@@ -358,7 +350,7 @@
         p = x + which * m
         done = (text_v[rows_of(p), :].astype(F32) + strength * branch).astype(BF16)
         fin[which] = done
-        for j in range(1, m):
+        for j in sorted(range(1, m), key=lambda j: -min(j, m - j)):
             f_copy(which, j).start()
         out_ref[rows_of(p), :] = done
 
@@ -376,7 +368,7 @@
                 if d <= tree_a.far(DIRS[i]):
                     at_copy(i, d).wait_recv()
         project(d)
-        if d == half - 1:
+        if d == max(half // 2, half - 2):
             finish_rows(early)
     finish_rows(1 - early)
 
@@ -410,8 +402,7 @@
 
 
 STEPS = (2, 2, 2, 2)
-BLOCK = 512
-UNROLL = 4
+BLOCK = 256
 
 
 def body(text, q_weight, out_weight, keys, values, gate):
@@ -425,13 +416,13 @@
     heads = wide // HD
     nq = heads * piece
     block = min(BLOCK, tokens)
-    unroll = min(UNROLL, tokens // block)
     trees = tuple(Tree(half, s) for s in STEPS)
     vm, dma = pltpu.VMEM, pltpu.SemaphoreType.DMA
     slots = (2, half + 1)
     scratch = [
         vm((rows, depth), BF16), vm((depth, wide), BF16), vm((wide, depth), BF16),
         vm((tokens, HD), BF16), vm((tokens, HD), BF16), vm((HD, tokens), BF16), dma((5,)),
+        vm((tokens, 2 * nq), F32),
         vm((rows, wide + HD), F32),
         vm((*slots, piece, wide + HD), BF16), vm((*slots, piece, wide + HD), BF16), dma(slots), dma(slots),
         vm((nq, HD), BF16), vm((half + 1, 2 * nq, HD), BF16), dma(slots), dma(slots),
@@ -444,13 +435,13 @@
     ]
     hbm = pl.BlockSpec(memory_space=pl.ANY)
     return pl.pallas_call(
-        functools.partial(kernel, (n, m, half, trees, block, unroll)),
+        functools.partial(kernel, (n, m, half, trees, block)),
         out_shape=jax.ShapeDtypeStruct((rows, depth), BF16),
         in_specs=[hbm] * 5 + [pl.BlockSpec(memory_space=pltpu.SMEM)],
         out_specs=pl.BlockSpec(memory_space=pltpu.VMEM),
         scratch_shapes=scratch,
         compiler_params=pltpu.CompilerParams(
-            collective_id=0, has_side_effects=True, vmem_limit_bytes=48 * 1024 * 1024
+            collective_id=0, has_side_effects=True, vmem_limit_bytes=67043328
         ),
     )(text, q_weight, out_weight, keys, values, gate)
 

time: 133 us -> 118 us (0.89)
  Pallas kernels: 126 us -> 116 us
  local copies, waits for them, and re-layouts: 6.55 us -> 1.67 us
    pallas_call x1, Pallas kernels: 126 us -> 116 us  [body(): pl.pallas_call(functools.partial(kernel, (n, m, half, trees, block)), out...]
    unnamed x11 -> x1, local copies, waits for them, and re-layouts: 6.55 us -> 1.67 us
where the time goes in v2:
time: 118 us
  Pallas kernels  116 us (98%)
  local copies, waits for them, and re-layouts  1.67 us (1%)
    pallas_call x1, Pallas kernels, body(): pl.pallas_call(functools.partial(kernel, (n, m, half, trees, block)), out...  116 us

profile of v2, /device:TPU:80, one launch (start us, length us, event | category | flops | bytes accessed | tf_op | source)
XLA Modules:
  0.0 118.1 jit_solution(1877315951762855057)
XLA Ops:
  0.7 115.8 %shard_map.64 = bf16[256,512]{1,0:T(8,128)(2,1)} custom-call(bf16[256,512]{1,0:T(8,128)(2,1)} %text_hbm.1, bf16[512,1024]{1,0:T(8,128)(2,1)} %q_hbm.1, bf16[1024,512]{1,0:T(8,128)(2,1)} %o_hbm.1, bf16[4096,128]{1,0:T(8,128)(2,1)} %k_hbm.1, bf16[4096,128]{1,0:T(8,128)(2,1)} %v_hbm.1, f32[1]{0:T(128)S(6)} %copy.8.gate_ref), custom_call_target="tpu_custom_call" | custom-call | tf_op jit(solution)/shard_map/pallas_call | solution.py:437
  116.5 1.7 %copy.9 = bf16[256,512]{1,0:T(8,128)(2,1)} copy(bf16[256,512]{1,0:T(8,128)(2,1)} %shard_map.64) | data formatting | bytes 524288

commit v3 on v2

--- a/solution.py
+++ b/solution.py
@@ -401,7 +401,7 @@
             f_copy(which, j).wait_send()
 
 
-STEPS = (2, 2, 2, 2)
+STEPS = (3, 2, 3, 2)
 BLOCK = 256
 
 

time: 118 us -> 119 us (level)
  no operation moved by 1% of the time
where the time goes in v3:
time: 119 us; the launch traced here: 118 us
  Pallas kernels  116 us (97%)
  local copies, waits for them, and re-layouts  1.67 us (1%)
    pallas_call x1, Pallas kernels, body(): pl.pallas_call(functools.partial(kernel, (n, m, half, trees, block)), out...  116 us

profile of v3, /device:TPU:80, one launch (start us, length us, event | category | flops | bytes accessed | tf_op | source)
XLA Modules:
  0.0 118.5 jit_solution(5466714984421834458)
XLA Ops:
  0.7 116.2 %shard_map.64 = bf16[256,512]{1,0:T(8,128)(2,1)} custom-call(bf16[256,512]{1,0:T(8,128)(2,1)} %text_hbm.1, bf16[512,1024]{1,0:T(8,128)(2,1)} %q_hbm.1, bf16[1024,512]{1,0:T(8,128)(2,1)} %o_hbm.1, bf16[4096,128]{1,0:T(8,128)(2,1)} %k_hbm.1, bf16[4096,128]{1,0:T(8,128)(2,1)} %v_hbm.1, f32[1]{0:T(128)S(6)} %copy.8.gate_ref), custom_call_target="tpu_custom_call" | custom-call | tf_op jit(solution)/shard_map/pallas_call | solution.py:437
  116.8 1.7 %copy.9 = bf16[256,512]{1,0:T(8,128)(2,1)} copy(bf16[256,512]{1,0:T(8,128)(2,1)} %shard_map.64) | data formatting | bytes 524288
